TPU v7x, 256 devices: a whole 4x4x8 slice. The times are simulated.
256 devices in a mesh: seq: 8 (over z), tensor: 8 (over x, y_hi), dp: 4 (over y_lo, core).
Axes of the slice: x: 4, y: 4 (y_hi: 2, y_lo: 2; y = y_hi * 2 + y_lo), z: 8, core: 2. Of those that a mesh axis runs over, the one named last changes fastest.
Arguments:
- tokens: bfloat16 [4, 2048, 3072], P('dp', 'seq'), may hold values from -6 to 6
- cotangent: bfloat16 [4, 2048, 3072], P('dp', 'seq'), may hold values from -6 to 6
- qkv_weight: bfloat16 [3072, 3, 3072], P(('seq', 'dp'), None, 'tensor'), may hold values from -0.109375 to 0.109375
- out_weight: bfloat16 [3072, 3072], P(('seq', 'dp'), 'tensor'), may hold values from -0.109375 to 0.109375
Outputs:
- qkv_grad: float32 [3072, 3, 3072], P(('seq', 'dp'), None, 'tensor')
- out_grad: float32 [3072, 3072], P(('seq', 'dp'), 'tensor')
- branch_grad: bfloat16 [4, 2048, 3072], P('dp', 'seq', 'tensor')
All inputs are finite; a program needn't handle non-finite values.
Results may differ from a plain program's by a relative error of at most 0.025.
Values may be sent and summed in bfloat16 or wider, within the bound.
No kernel may reach another device: no remote copies, remote signals or barrier semaphores. Data moves between devices by JAX's collectives and lax.ppermute only.
A program may use at most 128 MiB of HBM per device.

v0:
```python
import jax
import jax.numpy as jnp
from jax import lax
from jax.sharding import PartitionSpec as P

HD = 128
epsilon = 1e-06


def sent_together(arrays, axis, dim, along):
    both = jnp.concatenate(arrays, axis=along)
    result, at, done = (lax.all_gather(both, axis, axis=dim, tiled=True), 0, [])
    for a in arrays:
        done.append(lax.slice_in_dim(result, at, at + a.shape[along], axis=along))
        at += a.shape[along]
    return tuple(done)


def split_up(shard, dim, size):
    before, after = (shard.shape[:dim], shard.shape[dim + 1 :])
    return jnp.moveaxis(shard.reshape(*before, size, -1, *after), dim, 0)


def summed_on_arrival(shard, axis, dim):
    size = lax.axis_size(axis)
    pieces = lax.all_to_all(split_up(shard, dim, size), axis, 0, 0, tiled=True)
    return jnp.sum(pieces.astype(jnp.float32), axis=0)


def copy_for_each(shard, axis):
    copies = jnp.broadcast_to(shard, (lax.axis_size(axis), *shard.shape))
    return lax.all_to_all(copies, axis, split_axis=0, concat_axis=0, tiled=True)


def taken_together(shard, axis):
    everything = copy_for_each(shard, axis)
    return jnp.sum(everything, axis=0)


def in_one(arrays, axis):
    ends = [0]
    for a in arrays:
        ends.append(ends[-1] + a.size)
    subtotal = taken_together(jnp.concatenate([a.ravel() for a in arrays]), axis)
    return tuple((subtotal[b:e].reshape(a.shape) for a, b, e in zip(arrays, ends, ends[1:])))


def normalize(values):
    average = jnp.mean(values, axis=-1, keepdims=True)
    centered = values - average
    inverse = lax.rsqrt(jnp.mean(centered * centered, axis=-1, keepdims=True) + epsilon)
    return (centered * inverse, inverse)


def normalize_back(gradient, normed, inverse):
    mean_grad = jnp.mean(gradient, axis=-1, keepdims=True)
    mean_both = jnp.mean(gradient * normed, axis=-1, keepdims=True)
    return (gradient - mean_grad - normed * mean_both) * inverse


def local(tokens, cotangent, qkv_weight, out_weight):
    row_count = tokens.shape[1]
    feature_count = tokens.shape[2]
    column_count = out_weight.shape[1]
    head_count = column_count // HD
    score_scale = HD ** (-0.5)
    own_rows = qkv_weight.shape[0]
    grad_rows = cotangent[0]
    normed, inverse = normalize(tokens[0].astype(jnp.float32))
    unit_low = normed.astype(jnp.bfloat16)
    flat_weight = qkv_weight.reshape(own_rows, 3 * column_count)
    piece_qkv, piece_out = sent_together((flat_weight, out_weight), ("seq", "dp"), 0, 1)
    piece_rows = piece_qkv.shape[0]
    left_rows = unit_low
    right_rows = grad_rows
    projected = jnp.dot(left_rows, piece_qkv, preferred_element_type=jnp.float32)
    attended_grad = jnp.dot(right_rows, piece_out, preferred_element_type=jnp.float32)
    full_qkv = piece_qkv
    projected, attended_grad, full_qkv = (projected, attended_grad, full_qkv)
    query_unit, query_inv = normalize(
        projected[:, :column_count].reshape(row_count, head_count, HD)
    )
    key_unit, key_inv = normalize(
        projected[:, column_count : 2 * column_count].reshape(row_count, head_count, HD)
    )
    query_low = query_unit.astype(jnp.bfloat16)
    key_value = jnp.stack(
        [
            key_unit.astype(jnp.bfloat16).reshape(row_count, column_count),
            projected[:, 2 * column_count :].astype(jnp.bfloat16),
        ]
    )
    grad_low = attended_grad.astype(jnp.bfloat16).reshape(row_count, head_count, HD)

    def scores_of(key_rows):
        piece_rows = key_rows.shape[0]
        return (
            jnp.einsum(
                "qhd,khd->hqk",
                query_low,
                key_rows.reshape(piece_rows, head_count, HD),
                preferred_element_type=jnp.float32,
            )
            * score_scale
        )

    every_pair = lax.all_gather(key_value, "seq", axis=1, tiled=True)
    piece_rows = every_pair.shape[1]
    exponent = jnp.exp(scores_of(every_pair[0]))
    add_exp_total = jnp.sum(exponent, axis=-1)
    weighted = jnp.einsum(
        "hqk,khd->qhd",
        exponent.astype(jnp.bfloat16),
        every_pair[1].reshape(piece_rows, head_count, HD),
        preferred_element_type=jnp.float32,
    )
    exp_total, weighted = (add_exp_total, weighted)
    attended_low = (weighted / exp_total.T[:, :, None]).astype(jnp.bfloat16)
    row_delta = jnp.sum(grad_low.astype(jnp.float32) * attended_low.astype(jnp.float32), axis=-1)
    piece_rows = every_pair.shape[1]
    key_rows = every_pair[0].reshape(piece_rows, head_count, HD)
    value_rows = every_pair[1].reshape(piece_rows, head_count, HD)
    probability = jnp.exp(scores_of(every_pair[0])) / exp_total[:, :, None]
    prob_grad = jnp.einsum("qhd,khd->hqk", grad_low, value_rows, preferred_element_type=jnp.float32)
    grad_score = (probability * (prob_grad - row_delta.T[:, :, None]) * score_scale).astype(
        jnp.bfloat16
    )
    query_part = jnp.einsum(
        "hqk,khd->qhd", grad_score, key_rows, preferred_element_type=jnp.float32
    )
    key_part = jnp.einsum("hqk,qhd->khd", grad_score, query_low, preferred_element_type=jnp.float32)
    value_part = jnp.einsum(
        "hqk,qhd->khd",
        probability.astype(jnp.bfloat16),
        grad_low,
        preferred_element_type=jnp.float32,
    )
    every_grad = jnp.stack(
        [key_part.reshape(piece_rows, column_count), value_part.reshape(piece_rows, column_count)]
    )
    pair_grad = lax.psum_scatter(
        every_grad.astype(jnp.bfloat16), "seq", scatter_dimension=1, tiled=True
    ).astype(jnp.float32)
    query_back = normalize_back(query_part, query_unit, query_inv)
    key_back = normalize_back(pair_grad[0].reshape(row_count, head_count, HD), key_unit, key_inv)
    qkv_low = jnp.concatenate(
        [
            query_back.reshape(row_count, column_count),
            key_back.reshape(row_count, column_count),
            pair_grad[1],
        ],
        axis=1,
    ).astype(jnp.bfloat16)
    inner_grad = jnp.einsum("rc,dc->rd", qkv_low, full_qkv, preferred_element_type=jnp.float32)
    attended_flat = attended_low.reshape(row_count, column_count)
    share_width = feature_count // lax.axis_size("tensor")
    own_share = summed_on_arrival(inner_grad.astype(jnp.bfloat16), "tensor", 1)
    offset = lax.axis_index("tensor") * share_width
    unit_own = lax.dynamic_slice_in_dim(normed, offset, share_width, 1)
    row_sums = in_one(
        (
            jnp.sum(own_share, axis=1, keepdims=True),
            jnp.sum(own_share * unit_own, axis=1, keepdims=True),
        ),
        "tensor",
    )
    branch = (
        own_share - row_sums[0] / feature_count - unit_own * (row_sums[1] / feature_count)
    ) * inverse
    left_rows = unit_low
    right_rows = grad_rows
    qkv_term = jnp.einsum(
        "rd,rc->dc", left_rows, qkv_low, preferred_element_type=jnp.float32
    ).reshape(lax.axis_size(("seq", "dp")) * own_rows, 3, column_count)
    out_term = jnp.einsum(
        "rd,rc->dc", right_rows, attended_flat, preferred_element_type=jnp.float32
    )
    summed = lax.psum_scatter(
        jnp.concatenate([qkv_term, out_term[:, None, :]], axis=1).astype(jnp.bfloat16),
        ("seq", "dp"),
        scatter_dimension=0,
        tiled=True,
    ).astype(jnp.float32)
    return (summed[:, :3], summed[:, 3], branch.astype(jnp.bfloat16)[None])


def solution(mesh):
    return jax.shard_map(
        local,
        mesh=mesh,
        in_specs=(
            P("dp", "seq", None),
            P("dp", "seq", None),
            P(("seq", "dp"), None, "tensor"),
            P(("seq", "dp"), "tensor"),
        ),
        out_specs=(
            P(("seq", "dp"), None, "tensor"),
            P(("seq", "dp"), "tensor"),
            P("dp", "seq", "tensor"),
        ),
        check_vma=False,
    )
```

profile of v0, /device:TPU:16, one launch (start us, length us, event | category | flops | bytes accessed | tf_op | source)
XLA Modules:
  0.0 414.2 jit_solution(13253095489150140398)
XLA Ops:
  12.4 73.2 %all-gather.3.cloned.1.call-done = bf16[3072,1536]{1,0:T(8,128)(2,1)} async-done(((bf16[96,1536]{1,0:T(8,128)(2,1)}), bf16[3072,1536]{1,0:T(8,128)(2,1)}) %all-gather.3.cloned.1.call-update) | async-done | bytes 9437200 | tf_op jit(solution)/shard_map/all_gather | solution.py:12
  85.5 5.3 %fusion.2 = f32[256,1152]{1,0:T(8,128)S(1)} fusion(bf16[3072,1536]{1,0:T(8,128)(2,1)} %all-gather.3.cloned.1.call-done, bf16[1,256,3072]{2,1,0:T(8,128)(2,1)S(1)} %copy-done.1, f32[256]{0:T(256)S(1)} %add_rsqrt_fusion.2, f32[256]{0:T(256)S(1)} %broadcast_multiply_fusion.6), kind=kOutput, calls=%fused_computation.5 | convolution fusion | flops 1815085056 | bytes 9832448 | tf_op jit(solution)/shard_map/dot_general | solution.py:76
  104.7 3.2 fusion.38
  107.8 40.1 %all-gather.5.cloned.1.call-done = bf16[2,2048,384]{2,1,0:T(8,128)(2,1)} async-done(((bf16[2,256,384]{2,1,0:T(8,128)(2,1)}), bf16[2,2048,384]{2,1,0:T(8,128)(2,1)}) %all-gather.5.cloned.1.call-update) | async-done | bytes 3145744 | tf_op jit(solution)/shard_map/all_gather | solution.py:107
  147.9 3.9 fusion.64
  151.8 2.6 copy.93
  154.4 2.6 copy.97
  157.0 2.8 fusion.6
  159.8 2.6 fusion.22
  164.3 2.5 multiply_convert_fusion
  170.2 2.6 copy.100
  172.8 2.6 copy.101
  175.4 3.9 pad_maximum_fusion.1
  179.5 3.6 fusion.63
  185.7 3.4 fusion.7
  189.0 36.0 %reduce-scatter.3.cloned.1.call-done = bf16[2,256,384]{2,1,0:T(8,128)(2,1)} async-done(((bf16[2,2048,384]{2,1,0:T(8,128)(2,1)}), bf16[2,256,384]{2,1,0:T(8,128)(2,1)}) %reduce-scatter.3.cloned.1.call-update) | async-done | bytes 393232 | tf_op jit(solution)/shard_map/reduce_scatter | solution.py:141
  240.8 5.7 %convolution_convert_fusion = bf16[3072,3,384]{2,0,1:T(8,128)(2,1)} fusion(bf16[3,384,256]{2,1,0:T(8,128)(2,1)} %bitcast.114, bf16[1,256,3072]{2,1,0:T(8,128)(2,1)S(1)} %copy-done.1, f32[256]{0:T(256)S(1)} %copy-done.14, f32[256]{0:T(256)S(1)} %copy-done.12), kind=kOutput, calls=%fused_computation.7 | convolution fusion | flops 1818624000 | bytes 9242624 | tf_op jit(solution)/shard_map/rd,rc->dc/dot_general | solution.py:172
  246.5 8.4 %pad_maximum_fusion = bf16[3072,4,384]{2,0,1:T(8,128)(2,1)} fusion(bf16[3072,1,384]{2,0,1:T(8,128)(2,1)} %fusion.7, bf16[3072,3,384]{2,0,1:T(8,128)(2,1)} %convolution_convert_fusion), kind=kLoop, calls=%fused_computation | loop fusion | flops 4718592 | bytes 18874368 | tf_op jit(solution)/shard_map/concatenate | solution.py:179
  255.9 5.3 %fusion.8 = bf16[256,3072]{1,0:T(8,128)(2,1)S(1)} fusion(bf16[3072,1536]{1,0:T(8,128)(2,1)} %all-gather.3.cloned.1.call-done, bf16[256,384]{1,0:T(8,128)(2,1)} %get-tuple-element.14, bf16[256,384]{1,0:T(8,128)(2,1)S(1)} %copy-done.8, bf16[256,384]{1,0:T(8,128)(2,1)S(1)} %copy-done.9), kind=kOutput, calls=%fused_computation.18 | convolution fusion | flops 1814495232 | bytes 9240576 | tf_op jit(solution)/shard_map/rc,dc->rd/dot_general | solution.py:154
  262.6 7.3 %all-to-all-start = ((bf16[8,256,384]{2,1,0:T(8,128)(2,1)}), bf16[8,256,384]{2,1,0:T(8,128)(2,1)}, u32[]{:S(2)}, u32[]{:S(2)}) async-start(bf16[8,256,384]{2,1,0:T(8,128)(2,1)} %bitcast.107), calls=%async_computation.2 | async-start | bytes 3145728 | tf_op jit(solution)/shard_map/all_to_all | solution.py:26
  269.9 2.3 fusion.14
  272.2 17.6 %all-to-all-done = bf16[8,256,384]{2,1,0:T(8,128)(2,1)} async-done(((bf16[8,256,384]{2,1,0:T(8,128)(2,1)}), bf16[8,256,384]{2,1,0:T(8,128)(2,1)}, u32[]{:S(2)}, u32[]{:S(2)}) %all-to-all-start) | async-done | bytes 1572896 | tf_op jit(solution)/shard_map/all_to_all | solution.py:26
  292.8 12.0 %all_to_all.11 = f32[8,1,512]{2,1,0:T(1,128)S(1)} all-to-all(f32[8,1,512]{2,1,0:T(1,128)S(1)} %broadcast_in_dim.8), channel_id=1, replica_groups=mesh['seq'=8,'tensor'=8,'dp'=4] {'tensor'}, dimensions={0} | all-to-all | bytes 32768 | tf_op jit(solution)/shard_map/all_to_all | solution.py:32
  306.7 97.6 %reduce-scatter.5.cloned.1.call-done = bf16[96,4,384]{2,0,1:T(8,128)(2,1)} async-done(((bf16[3072,4,384]{2,0,1:T(8,128)(2,1)}), bf16[96,4,384]{2,0,1:T(8,128)(2,1)}) %reduce-scatter.5.cloned.1.call-update) | async-done | bytes 294928 | tf_op jit(solution)/shard_map/reduce_scatter | solution.py:178
  (89 shorter events, 53.2 us)
Async XLA Ops:
  7.2 97.5 %copy-start = (bf16[1,256,3072]{2,1,0:T(8,128)(2,1)S(1)}, bf16[1,256,3072]{2,1,0:T(8,128)(2,1)}, u32[]{:S(2)}) copy-start(bf16[1,256,3072]{2,1,0:T(8,128)(2,1)} %param.5) | copy-start | bytes 4718596
  7.2 4.6 %copy-start.1 = (bf16[1,256,3072]{2,1,0:T(8,128)(2,1)S(1)}, bf16[1,256,3072]{2,1,0:T(8,128)(2,1)}, u32[]{:S(2)}) copy-start(bf16[1,256,3072]{2,1,0:T(8,128)(2,1)} %param.4) | copy-start | bytes 4718596
  7.2 78.3 %all-gather.3.cloned.1.call-start = ((), (), s32[]{:S(2)}) async-start(), calls=%async_computation.4 | async-start | bytes 9732096 | tf_op jit(solution)/shard_map/all_gather | solution.py:12
  10.0 137.9 %all-gather.5.cloned.1.call-start = ((), (), s32[]{:S(2)}) async-start(), calls=%async_computation.5 | async-start | bytes 3538944 | tf_op jit(solution)/shard_map/all_gather | solution.py:107
  11.8 79.0 %copy-start.11 = (f32[256]{0:T(256)}, f32[256]{0:T(256)S(1)}, u32[]{:S(2)}) copy-start(f32[256]{0:T(256)S(1)} %broadcast_multiply_fusion.6) | copy-start | bytes 3076
  12.3 78.4 %copy-start.13 = (f32[256]{0:T(256)}, f32[256]{0:T(256)S(1)}, u32[]{:S(2)}) copy-start(f32[256]{0:T(256)S(1)} %add_rsqrt_fusion.2) | copy-start | bytes 3076
  90.8 1.2 copy-start.6
  93.8 9.5 %copy-start.4 = (f32[256,384]{0,1:T(8,128)}, f32[256,384]{0,1:T(8,128)S(1)}, u32[]{:S(2)}) copy-start(f32[256,384]{0,1:T(8,128)S(1)} %copy.90) | copy-start | bytes 1179652
  103.3 121.7 %reduce-scatter.3.cloned.1.call-start = ((), (), s32[]{:S(2)}) async-start(), calls=%async_computation.6 | async-start | bytes 3538944 | tf_op jit(solution)/shard_map/reduce_scatter | solution.py:141
  157.0 2.8 copy-start.10
  159.8 2.6 copy-start.3
  166.8 1.6 copy-start.2
  179.3 225.0 %reduce-scatter.5.cloned.1.call-start = ((), (), s32[]{:S(2)}) async-start(), calls=%async_computation.7 | async-start | bytes 9732096 | tf_op jit(solution)/shard_map/reduce_scatter | solution.py:178
  183.9 44.9 %copy-start.5 = (f32[256,384]{0,1:T(8,128)S(1)}, f32[256,384]{0,1:T(8,128)}, u32[]{:S(2)}) copy-start(f32[256,384]{0,1:T(8,128)} %copy-done.4) | copy-start | bytes 1179652
  231.9 8.9 %copy-start.12 = (f32[256]{0:T(256)S(1)}, f32[256]{0:T(256)}, u32[]{:S(2)}) copy-start(f32[256]{0:T(256)} %copy-done.11) | copy-start | bytes 3076
  231.9 8.9 %copy-start.14 = (f32[256]{0:T(256)S(1)}, f32[256]{0:T(256)}, u32[]{:S(2)}) copy-start(f32[256]{0:T(256)} %copy-done.13) | copy-start | bytes 3076
  236.1 0.7 copy-start.7
  254.9 0.9 copy-start.8
  254.9 1.0 copy-start.9
  262.6 27.2 %all-to-all-start = ((bf16[8,256,384]{2,1,0:T(8,128)(2,1)}), bf16[8,256,384]{2,1,0:T(8,128)(2,1)}, u32[]{:S(2)}, u32[]{:S(2)}) async-start(bf16[8,256,384]{2,1,0:T(8,128)(2,1)} %bitcast.107), calls=%async_computation.2 | async-start | bytes 3145728 | tf_op jit(solution)/shard_map/all_to_all | solution.py:26
Sparse Core Ops, SparseCore 0:
  10.4 75.0 all-gather.2
  103.4 44.4 all-gather.4
  179.4 45.5 reduce-scatter.2
  255.1 149.1 reduce-scatter.4
where the time goes:
time: 415 us; the launch traced here: 414 us
  waiting for transfers between devices  264 us (64%)
  local copies, waits for them, and re-layouts  42.5 us (10%)
  matrix products  37.9 us (9%)
  other arithmetic  35.6 us (9%)
  between operations  14 us (3%)
  blocking collectives  12 us (3%)
  starting transfers between devices  7.64 us (2%)
    reduce_scatter x1, waiting for transfers between devices, local(): lax.psum_scatter(jnp.concatenate([qkv_term, out_term[:, None, :]], axis=1...  97.6 us
    all_gather x1, waiting for transfers between devices, sent_together(): result, at, done = (lax.all_gather(both, axis, axis=dim, tiled=True), 0, [])  73.2 us
    all_gather x1, waiting for transfers between devices, local(): every_pair = lax.all_gather(key_value, 'seq', axis=1, tiled=True)  40.1 us
    reduce_scatter x1, waiting for transfers between devices, local(): lax.psum_scatter(every_grad.astype(jnp.bfloat16), 'seq', scatter_dimensio...  36 us
    all_to_all x1, waiting for transfers between devices, summed_on_arrival(): pieces = lax.all_to_all(split_up(shard, dim, size), axis, 0, 0, tiled=True)  17.6 us
    all_to_all x1, blocking collectives, copy_for_each(): return lax.all_to_all(copies, axis, split_axis=0, concat_axis=0, tiled=True)  12 us
    concatenate x1, other arithmetic, local(): jnp.concatenate([qkv_term, out_term[:, None, :]], axis=1)  8.45 us
  transfers between devices with their start and end apart: 5, of which 5 were waited for; matrix products, arithmetic and copies ran while one was open for 7% of the time, Pallas kernels for 0%

commit v1 on v0

--- a/solution.py
+++ b/solution.py
@@ -5,6 +5,13 @@
 
 HD = 128
 epsilon = 1e-06
+
+
+def all_by_exchange(x, axis, along):
+    peers = lax.axis_size(axis)
+    blocks = jnp.stack([x for _ in range(peers)])
+    blocks = lax.all_to_all(blocks, axis, split_axis=0, concat_axis=0)
+    return jnp.concatenate(blocks, axis=along)
 
 
 def sent_together(arrays, axis, dim, along):
@@ -104,7 +111,7 @@
             * score_scale
         )
 
-    every_pair = lax.all_gather(key_value, "seq", axis=1, tiled=True)
+    every_pair = all_by_exchange(key_value, "seq", 1)
     piece_rows = every_pair.shape[1]
     exponent = jnp.exp(scores_of(every_pair[0]))
     add_exp_total = jnp.sum(exponent, axis=-1)

time: 415 us -> 461 us (1.11)
  waiting for transfers between devices: 264 us -> 292 us
  local copies, waits for them, and re-layouts: 42.5 us -> 54.6 us
  starting transfers between devices: 7.64 us -> 12.7 us
    all_to_all x0 -> x1, waiting for transfers between devices: none -> 69.6 us  [all_by_exchange(): blocks = lax.all_to_all(blocks, axis, split_axis=0, concat_axis=0)]
    all_gather x1 -> x0, waiting for transfers between devices: 40.1 us -> none  [local(): every_pair = lax.all_gather(key_value, 'seq', axis=1, tiled=True)]
    another operation x0 -> x3, local copies, waits for them, and re-layouts: none -> 10.5 us  [the longest x1 3.77 us: local(): value_rows = every_pair[1].reshape(piece_rows, head_count, HD)]
    all_to_all x0 -> x1, starting transfers between devices: none -> 5 us  [all_by_exchange(): blocks = lax.all_to_all(blocks, axis, split_axis=0, concat_axis=0)]
where the time goes in v1:
time: 461 us; the launch traced here: 458 us
  waiting for transfers between devices  292 us (63%)
  local copies, waits for them, and re-layouts  54.6 us (12%)
  matrix products  37.9 us (8%)
  other arithmetic  35.6 us (8%)
  between operations  14 us (3%)
  starting transfers between devices  12.7 us (3%)
  blocking collectives  11.8 us (3%)
    reduce_scatter x1, waiting for transfers between devices, local(): lax.psum_scatter(jnp.concatenate([qkv_term, out_term[:, None, :]], axis=1...  97.4 us
    all_gather x1, waiting for transfers between devices, sent_together(): result, at, done = (lax.all_gather(both, axis, axis=dim, tiled=True), 0, [])  73.2 us
    all_to_all x1, waiting for transfers between devices, all_by_exchange(): blocks = lax.all_to_all(blocks, axis, split_axis=0, concat_axis=0)  69.6 us
    reduce_scatter x1, waiting for transfers between devices, local(): lax.psum_scatter(every_grad.astype(jnp.bfloat16), 'seq', scatter_dimensio...  33.8 us
    all_to_all x1, waiting for transfers between devices, summed_on_arrival(): pieces = lax.all_to_all(split_up(shard, dim, size), axis, 0, 0, tiled=True)  17.7 us
    all_to_all x1, blocking collectives, copy_for_each(): return lax.all_to_all(copies, axis, split_axis=0, concat_axis=0, tiled=True)  11.8 us
  transfers between devices with their start and end apart: 5, of which 5 were waited for; matrix products, arithmetic and copies ran while one was open for 7% of the time, Pallas kernels for 0%

profile of v1, /device:TPU:16, one launch (start us, length us, event | category | flops | bytes accessed | tf_op | source)
XLA Modules:
  0.0 458.3 jit_solution(9835672840156518721)
XLA Ops:
  12.3 73.2 %all-gather.2.cloned.1.call-done = bf16[3072,1536]{1,0:T(8,128)(2,1)} async-done(((bf16[96,1536]{1,0:T(8,128)(2,1)}), bf16[3072,1536]{1,0:T(8,128)(2,1)}) %all-gather.2.cloned.1.call-update) | async-done | bytes 9437200 | tf_op jit(solution)/shard_map/all_gather | solution.py:19
  85.5 5.3 %fusion.2 = f32[256,1152]{1,0:T(8,128)S(1)} fusion(bf16[3072,1536]{1,0:T(8,128)(2,1)} %all-gather.2.cloned.1.call-done, bf16[1,256,3072]{2,1,0:T(8,128)(2,1)S(1)} %copy-done.1, f32[256]{0:T(256)S(1)} %add_rsqrt_fusion.2, f32[256]{0:T(256)S(1)} %broadcast_multiply_fusion.6), kind=kOutput, calls=%fused_computation.5 | convolution fusion | flops 1815085056 | bytes 9832448 | tf_op jit(solution)/shard_map/dot_general | solution.py:83
  105.2 3.0 stack.11
  108.1 5.0 %all-to-all-start = ((bf16[8,2,256,384]{2,3,1,0:T(8,128)(2,1)}), bf16[8,2,256,384]{2,3,1,0:T(8,128)(2,1)}, u32[]{:S(2)}, u32[]{:S(2)}) async-start(bf16[8,2,256,384]{2,3,1,0:T(8,128)(2,1)} %stack.11), calls=%async_computation | async-start | bytes 6291456 | tf_op jit(solution)/shard_map/all_to_all | solution.py:13
  114.7 3.2 fusion.38
  117.8 69.6 %all-to-all-done = bf16[8,2,256,384]{2,3,1,0:T(8,128)(2,1)} async-done(((bf16[8,2,256,384]{2,3,1,0:T(8,128)(2,1)}), bf16[8,2,256,384]{2,3,1,0:T(8,128)(2,1)}, u32[]{:S(2)}, u32[]{:S(2)}) %all-to-all-start) | async-done | bytes 3145760 | tf_op jit(solution)/shard_map/all_to_all | solution.py:13
  187.4 3.4 fusion.64
  192.8 3.7 reshape_squeeze.14
  196.6 3.4 copy.97
  200.0 3.8 reshape_squeeze.15
  203.8 2.8 fusion.6
  206.6 2.6 fusion.22
  216.9 2.6 copy.100
  222.1 3.9 pad_maximum_fusion.1
  226.3 3.6 fusion.63
  232.5 3.4 fusion.7
  235.8 33.8 %reduce-scatter.3.cloned.1.call-done = bf16[2,256,384]{2,1,0:T(8,128)(2,1)} async-done(((bf16[2,2048,384]{2,1,0:T(8,128)(2,1)}), bf16[2,256,384]{2,1,0:T(8,128)(2,1)}) %reduce-scatter.3.cloned.1.call-update) | async-done | bytes 393232 | tf_op jit(solution)/shard_map/reduce_scatter | solution.py:148
  285.4 5.7 %convolution_convert_fusion = bf16[3072,3,384]{2,0,1:T(8,128)(2,1)} fusion(bf16[3,384,256]{2,1,0:T(8,128)(2,1)} %bitcast.117, bf16[1,256,3072]{2,1,0:T(8,128)(2,1)S(1)} %copy-done.1, f32[256]{0:T(256)S(1)} %copy-done.14, f32[256]{0:T(256)S(1)} %copy-done.12), kind=kOutput, calls=%fused_computation.7 | convolution fusion | flops 1818624000 | bytes 9242624 | tf_op jit(solution)/shard_map/rd,rc->dc/dot_general | solution.py:179
  291.1 8.4 %pad_maximum_fusion = bf16[3072,4,384]{2,0,1:T(8,128)(2,1)} fusion(bf16[3072,1,384]{2,0,1:T(8,128)(2,1)} %fusion.7, bf16[3072,3,384]{2,0,1:T(8,128)(2,1)} %convolution_convert_fusion), kind=kLoop, calls=%fused_computation | loop fusion | flops 4718592 | bytes 18874368 | tf_op jit(solution)/shard_map/concatenate | solution.py:186
  300.5 5.3 %fusion.8 = bf16[256,3072]{1,0:T(8,128)(2,1)S(1)} fusion(bf16[3072,1536]{1,0:T(8,128)(2,1)} %all-gather.2.cloned.1.call-done, bf16[256,384]{1,0:T(8,128)(2,1)} %get-tuple-element.14, bf16[256,384]{1,0:T(8,128)(2,1)S(1)} %copy-done.8, bf16[256,384]{1,0:T(8,128)(2,1)S(1)} %copy-done.9), kind=kOutput, calls=%fused_computation.18 | convolution fusion | flops 1814495232 | bytes 9240576 | tf_op jit(solution)/shard_map/rc,dc->rd/dot_general | solution.py:161
  307.2 7.2 %all-to-all-start.1 = ((bf16[8,256,384]{2,1,0:T(8,128)(2,1)}), bf16[8,256,384]{2,1,0:T(8,128)(2,1)}, u32[]{:S(2)}, u32[]{:S(2)}) async-start(bf16[8,256,384]{2,1,0:T(8,128)(2,1)} %bitcast.112), calls=%async_computation.3 | async-start | bytes 3145728 | tf_op jit(solution)/shard_map/all_to_all | solution.py:33
  316.7 17.7 %all-to-all-done.1 = bf16[8,256,384]{2,1,0:T(8,128)(2,1)} async-done(((bf16[8,256,384]{2,1,0:T(8,128)(2,1)}), bf16[8,256,384]{2,1,0:T(8,128)(2,1)}, u32[]{:S(2)}, u32[]{:S(2)}) %all-to-all-start.1) | async-done | bytes 1572896 | tf_op jit(solution)/shard_map/all_to_all | solution.py:33
  337.4 11.8 %all_to_all.16 = f32[8,1,512]{2,1,0:T(1,128)S(1)} all-to-all(f32[8,1,512]{2,1,0:T(1,128)S(1)} %broadcast_in_dim.8), channel_id=1, replica_groups=mesh['seq'=8,'tensor'=8,'dp'=4] {'tensor'}, dimensions={0} | all-to-all | bytes 32768 | tf_op jit(solution)/shard_map/all_to_all | solution.py:39
  351.0 97.4 %reduce-scatter.5.cloned.1.call-done = bf16[96,4,384]{2,0,1:T(8,128)(2,1)} async-done(((bf16[3072,4,384]{2,0,1:T(8,128)(2,1)}), bf16[96,4,384]{2,0,1:T(8,128)(2,1)}) %reduce-scatter.5.cloned.1.call-update) | async-done | bytes 294928 | tf_op jit(solution)/shard_map/reduce_scatter | solution.py:185
  (92 shorter events, 64.6 us)
Async XLA Ops:
  7.2 107.5 %copy-start = (bf16[1,256,3072]{2,1,0:T(8,128)(2,1)S(1)}, bf16[1,256,3072]{2,1,0:T(8,128)(2,1)}, u32[]{:S(2)}) copy-start(bf16[1,256,3072]{2,1,0:T(8,128)(2,1)} %param.5) | copy-start | bytes 4718596
  7.2 4.5 copy-start.1
  7.2 78.3 %all-gather.2.cloned.1.call-start = ((), (), s32[]{:S(2)}) async-start(), calls=%async_computation.5 | async-start | bytes 9732096 | tf_op jit(solution)/shard_map/all_gather | solution.py:19
  11.7 79.1 %copy-start.11 = (f32[256]{0:T(256)}, f32[256]{0:T(256)S(1)}, u32[]{:S(2)}) copy-start(f32[256]{0:T(256)S(1)} %broadcast_multiply_fusion.6) | copy-start | bytes 3076
  12.3 78.5 %copy-start.13 = (f32[256]{0:T(256)}, f32[256]{0:T(256)S(1)}, u32[]{:S(2)}) copy-start(f32[256]{0:T(256)S(1)} %add_rsqrt_fusion.2) | copy-start | bytes 3076
  90.8 1.2 copy-start.6
  93.8 11.3 %copy-start.4 = (f32[256,384]{0,1:T(8,128)}, f32[256,384]{0,1:T(8,128)S(1)}, u32[]{:S(2)}) copy-start(f32[256,384]{0,1:T(8,128)S(1)} %copy.89) | copy-start | bytes 1179652
  108.1 79.3 %all-to-all-start = ((bf16[8,2,256,384]{2,3,1,0:T(8,128)(2,1)}), bf16[8,2,256,384]{2,3,1,0:T(8,128)(2,1)}, u32[]{:S(2)}, u32[]{:S(2)}) async-start(bf16[8,2,256,384]{2,3,1,0:T(8,128)(2,1)} %stack.11), calls=%async_computation | async-start | bytes 6291456 | tf_op jit(solution)/shard_map/all_to_all | solution.py:13
  113.1 156.5 %reduce-scatter.3.cloned.1.call-start = ((), (), s32[]{:S(2)}) async-start(), calls=%async_computation.6 | async-start | bytes 3538944 | tf_op jit(solution)/shard_map/reduce_scatter | solution.py:148
  203.8 2.8 copy-start.10
  206.6 2.6 copy-start.3
  213.5 1.6 copy-start.2
  226.1 222.4 %reduce-scatter.5.cloned.1.call-start = ((), (), s32[]{:S(2)}) async-start(), calls=%async_computation.7 | async-start | bytes 9732096 | tf_op jit(solution)/shard_map/reduce_scatter | solution.py:185
  230.7 42.7 %copy-start.5 = (f32[256,384]{0,1:T(8,128)S(1)}, f32[256,384]{0,1:T(8,128)}, u32[]{:S(2)}) copy-start(f32[256,384]{0,1:T(8,128)} %copy-done.4) | copy-start | bytes 1179652
  276.5 8.9 %copy-start.12 = (f32[256]{0:T(256)S(1)}, f32[256]{0:T(256)}, u32[]{:S(2)}) copy-start(f32[256]{0:T(256)} %copy-done.11) | copy-start | bytes 3076
  276.5 8.9 %copy-start.14 = (f32[256]{0:T(256)S(1)}, f32[256]{0:T(256)}, u32[]{:S(2)}) copy-start(f32[256]{0:T(256)} %copy-done.13) | copy-start | bytes 3076
  280.7 0.7 copy-start.7
  299.5 0.9 copy-start.8
  299.5 1.0 copy-start.9
  307.2 27.2 %all-to-all-start.1 = ((bf16[8,256,384]{2,1,0:T(8,128)(2,1)}), bf16[8,256,384]{2,1,0:T(8,128)(2,1)}, u32[]{:S(2)}, u32[]{:S(2)}) async-start(bf16[8,256,384]{2,1,0:T(8,128)(2,1)} %bitcast.112), calls=%async_computation.3 | async-start | bytes 3145728 | tf_op jit(solution)/shard_map/all_to_all | solution.py:33
Sparse Core Ops, SparseCore 0:
  10.4 75.0 all-gather.1
  226.2 43.4 reduce-scatter.2
  299.7 148.6 reduce-scatter.4
